TPU v7x, 32 devices: a whole 2x2x4 slice. The times are simulated.
32 devices in a mesh: rep: 2 (over y), span: 2 (over core), seq: 4 (over z), tp: 2 (over x).
Axes of the slice: x: 2, y: 2, z: 4, core: 2. Of those that a mesh axis runs over, the one named last changes fastest.
Arguments:
- queries: bfloat16 [8, 512, 24, 128], P(('rep', 'span'), 'seq', 'tp'), parts along dimension 0, may hold values from -110 to 110
- key_states: bfloat16 [8, 512, 4, 128], P(('rep', 'span'), 'seq', 'tp'), parts along dimension 0, may hold values from -11 to 11
- value_states: bfloat16 [8, 512, 4, 128], P(('rep', 'span'), 'seq', 'tp'), parts along dimension 0, may hold values from -6 to 6
- out_weight: bfloat16 [3072, 6144], P('tp', 'seq'), may hold values from -0.109375 to 0.109375
- noise_table: float32 [64, 6144], P(None, 'tp'), may hold values from 0.5 to 2
- plan: int32 [8], P('rep'), parts along dimension 0, may hold values from 0 to 63
Outputs:
- branch_out: bfloat16 [8, 512, 6144], P(('rep', 'span'), 'seq', 'tp'), parts along dimension 0
There are 2 independent parts, one for each index of `rep`. A program takes and returns all parts, laid end to end along the dimension named above; an argument that names none is the same for every part. Nothing has to cross between parts.
All inputs are finite; a program needn't handle non-finite values.
Results may differ from a plain program's by a relative error of at most 0.014.
Values may be sent and summed in bfloat16 or wider, within the bound.
A program may use at most 128 MiB of HBM per device.

v0:
```python
import jax
import jax.numpy as jnp
from jax import lax
from jax.sharding import PartitionSpec as P


def fold_block(carried, query_rows, key_rows, value_rows, factor):
    maxima, totals, weighted = carried
    scores = (
        jnp.einsum("tkgd,skd->tkgs", query_rows, key_rows, preferred_element_type=jnp.float32)
        * factor
    )
    highest = jnp.maximum(maxima, jnp.max(scores, axis=-1))
    shrink = jnp.exp(maxima - highest)
    weights = jnp.exp(scores - highest[..., None])
    totals = totals * shrink + jnp.sum(weights, axis=-1)
    weighted = weighted * shrink[..., None] + jnp.einsum(
        "tkgs,skd->tkgd",
        weights.astype(jnp.bfloat16),
        value_rows,
        preferred_element_type=jnp.float32,
    )
    return (maxima * 0.0 + highest, totals, weighted)


def per_device(queries, key_states, value_states, out_weight, noise_table, plan):
    ch_dev, tok_dev, heads_local, head_size = queries.shape
    kv_local = key_states.shape[2]
    per_kv = heads_local // kv_local
    span_count = ch_dev * lax.axis_size("span")
    first_span = lax.axis_index("span") * ch_dev
    factor = head_size ** (-0.5)
    grouped = queries.reshape(ch_dev, tok_dev, kv_local, per_kv, head_size)
    start_max = jnp.full((ch_dev, tok_dev, kv_local, per_kv), -1e30, jnp.float32)
    start_tot = jnp.zeros((ch_dev, tok_dev, kv_local, per_kv), jnp.float32)
    start_acc = jnp.zeros((ch_dev, tok_dev, kv_local, per_kv, head_size), jnp.float32)
    span_rows = (
        lax.all_gather(key_states, "seq", axis=1, tiled=True),
        lax.all_gather(value_states, "seq", axis=1, tiled=True),
    )
    key_piece = lax.all_gather(span_rows[0], "span", axis=0, tiled=True)
    value_piece = lax.all_gather(span_rows[1], "span", axis=0, tiled=True)
    new_max = []
    new_tot = []
    new_acc = []
    for q_span in range(ch_dev):
        inner_state = (start_max[q_span], start_tot[q_span], start_acc[q_span])
        for k_span in range(span_count):

            def update(inner, q_span=q_span, k_span=k_span):
                return fold_block(
                    inner, grouped[q_span], key_piece[k_span], value_piece[k_span], factor
                )

            inner_state = lax.cond(
                k_span <= first_span + q_span, update, lambda inner: inner, inner_state
            )
        new_max.append(inner_state[0])
        new_tot.append(inner_state[1])
        new_acc.append(inner_state[2])
    attn = (
        (jnp.stack(new_acc) / jnp.stack(new_tot)[..., None])
        .reshape(ch_dev, tok_dev, heads_local * head_size)
        .astype(jnp.bfloat16)
    )
    columns = jnp.einsum(
        "ctf,fo->cto",
        lax.all_gather(attn, "seq", axis=1, tiled=True),
        out_weight,
        preferred_element_type=jnp.float32,
    )
    partial_out = lax.all_to_all(
        columns.astype(jnp.bfloat16), "seq", split_axis=1, concat_axis=2, tiled=True
    ).astype(columns.dtype)
    summed = lax.psum_scatter(
        partial_out.astype(jnp.bfloat16), "tp", scatter_dimension=2, tiled=True
    ).astype(jnp.float32)
    levels = lax.dynamic_slice_in_dim(plan, first_span, ch_dev)
    picks = (levels[:, None] == jnp.arange(noise_table.shape[0], dtype=jnp.int32)[None, :]).astype(
        jnp.float32
    )
    gates = jnp.dot(picks, noise_table, precision=lax.Precision.HIGHEST)
    return (summed * gates[:, None, :]).astype(jnp.bfloat16)


def solution(mesh):
    placed = (
        P(("rep", "span"), "seq", "tp", None),
        P(("rep", "span"), "seq", "tp", None),
        P(("rep", "span"), "seq", "tp", None),
        P("tp", "seq"),
        P(None, "tp"),
        P("rep"),
    )
    return jax.shard_map(
        per_device,
        mesh=mesh,
        in_specs=placed,
        out_specs=P(("rep", "span"), "seq", "tp"),
        check_vma=False,
    )
```

profile of v0, /device:TPU:0, one launch (start us, length us, event | category | flops | bytes accessed | tf_op | source)
XLA Modules:
  0.0 320.5 jit_solution(18199733619609409647)
XLA Ops:
  6.5 1.0 copy.63
  7.5 18.0 %all_gather.15 = bf16[2,512,2,128]{3,1,2,0:T(8,128)(2,1)} all-gather(bf16[2,128,2,128]{3,1,2,0:T(8,128)(2,1)S(1)} %copy.63), channel_id=1, replica_groups=mesh['rep'=2,'span'=2,'seq'=4,'tp'=2] {'seq'}, dimensions={1}, use_global_device_ids=true | all-gather | bytes 655360 | tf_op jit(solution)/shard_map/all_gather | solution.py:38
  25.6 0.9 copy.64
  26.5 17.0 %all_gather.17 = bf16[2,512,2,128]{3,1,2,0:T(8,128)(2,1)} all-gather(bf16[2,128,2,128]{3,1,2,0:T(8,128)(2,1)S(1)} %copy.64), channel_id=1, replica_groups=mesh['rep'=2,'span'=2,'seq'=4,'tp'=2] {'seq'}, dimensions={1}, use_global_device_ids=true | all-gather | bytes 655360 | tf_op jit(solution)/shard_map/all_gather | solution.py:39
  43.7 9.6 %all-gather.6.cloned.1.call-done = bf16[4,512,2,128]{3,1,2,0:T(8,128)(2,1)} async-done(((bf16[2,512,2,128]{3,1,2,0:T(8,128)(2,1)}), bf16[4,512,2,128]{3,1,2,0:T(8,128)(2,1)}) %all-gather.6.cloned.1.call-update) | async-done | bytes 1048592 | tf_op jit(solution)/shard_map/all_gather | solution.py:42
  53.3 6.1 %conditional.12 = (f32[128,2,6]{0,2,1:T(8,128)}, f32[128,2,6]{0,2,1:T(8,128)S(1)}, f32[128,2,6,128]{3,0,2,1:T(8,128)S(1)}) conditional(s32[]{:T(128)} %convert_element_type.70, () %tuple.93, (bf16[4,512,2,128]{3,1,2,0:T(8,128)(2,1)}, bf16[2,128,2,6,128]{4,1,3,2,0:T(8,128)(2,1)}, bf16[4,512,2,128]{3,1,2,0:T(8,128)(2,1)}) %tuple.190), branch_computations={%region_16.0_spmd, %region_17.0_spmd} | conditional | flops 409147392 | bytes 11210776 | solution.py:55
  53.3 1.7 bitcast_reduce_fusion.4
  55.6 1.2 fusion.85
  56.8 0.7 fusion.104
  57.5 1.9 fusion.93
  59.4 6.2 %conditional.13 = ((f32[128,2,6]{0,2,1:T(8,128)}, f32[128,2,6]{0,2,1:T(8,128)S(1)}, f32[128,2,6,128]{3,0,2,1:T(8,128)S(1)})) conditional(s32[]{:T(128)} %convert_element_type.69, (f32[128,2,6]{0,2,1:T(8,128)}, f32[128,2,6]{0,2,1:T(8,128)S(1)}, f32[128,2,6,128]{3,0,2,1:T(8,128)S(1)}) %conditional.12, (f32[128,2,6]{0,2,1:T(8,128)}, ...), branch_computations={%region_20.0_spmd, %region_21.0_spmd} | conditional | flops 409344000 | bytes 12032032 | solution.py:55
  59.4 1.7 bitcast_reduce_fusion.5
  62.3 0.7 multiply_add_fusion.4
  63.6 2.0 fusion.115
  65.6 6.1 %conditional.8 = (f32[128,2,6]{0,2,1:T(8,128)}, f32[128,2,6]{0,2,1:T(8,128)S(1)}, f32[128,2,6,128]{3,0,2,1:T(8,128)S(1)}) conditional(s32[]{:T(128)} %convert_element_type.66, () %tuple.87, (bf16[4,512,2,128]{3,1,2,0:T(8,128)(2,1)}, bf16[2,128,2,6,128]{4,1,3,2,0:T(8,128)(2,1)}, bf16[4,512,2,128]{3,1,2,0:T(8,128)(2,1)}) %tuple.193), branch_computations={%region_0.0_spmd, %region_1.0_spmd} | conditional | flops 409147392 | bytes 11210776 | solution.py:55
  65.6 1.7 bitcast_reduce_fusion
  67.9 1.2 fusion.2
  69.8 1.9 fusion.10
  72.0 1.5 conditional.15
  72.2 1.2 copy.102
  73.4 1.4 conditional.11
  73.7 1.2 copy.100
  75.0 1.6 copy.73
  76.6 2.9 fusion.171
  79.6 93.0 %all-gather.8.cloned.1.call-done = bf16[2,512,1536]{2,1,0:T(8,128)(2,1)} async-done(((bf16[2,128,1536]{2,1,0:T(8,128)(2,1)}), bf16[2,512,1536]{2,1,0:T(8,128)(2,1)}) %all-gather.8.cloned.1.call-update) | async-done | bytes 3145744 | tf_op jit(solution)/shard_map/all_gather | solution.py:68
  172.6 8.1 %fusion.168 = bf16[2,512,1536]{2,1,0:T(8,128)(2,1)S(1)} fusion(bf16[2,512,1536]{2,1,0:T(8,128)(2,1)} %all-gather.8.cloned.1.call-done, bf16[1536,1536]{1,0:T(8,128)(2,1)} %param.25), kind=kOutput, calls=%fused_computation.166 | convolution fusion | flops 4833411072 | bytes 11010048 | tf_op jit(solution)/shard_map/ctf,fo->cto/dot_general | solution.py:66
  180.7 3.2 %copy.74 = bf16[2,512,1536]{2,0,1:T(2,128)(2,1)S(1)} copy(bf16[2,512,1536]{2,1,0:T(8,128)(2,1)S(1)} %fusion.168) | data formatting | bytes 6291456 | tf_op jit(solution)/shard_map/convert_element_type | solution.py:73
  183.9 73.3 %all_to_all.18 = bf16[2,512,1536]{2,0,1:T(2,128)(2,1)S(1)} all-to-all(bf16[2,512,1536]{2,0,1:T(2,128)(2,1)S(1)} %copy.74), channel_id=1, replica_groups=mesh['rep'=2,'span'=2,'seq'=4,'tp'=2] {'seq'}, dimensions={1} | all-to-all | bytes 6291456 | tf_op jit(solution)/shard_map/all_to_all | solution.py:72
  257.2 4.1 %copy.75 = bf16[2,128,4,1536]{3,2,1,0:T(4,128)(2,1)} copy(bf16[2,128,4,1536]{3,0,1,2:T(2,128)(2,1)S(1)} %bitcast.326) | data formatting | bytes 6291456 | tf_op jit(solution)/shard_map/all_to_all | solution.py:72
  261.3 6.9 %all_to_all.16 = bf16[2,128,6144]{2,1,0:T(8,128)(2,1)} reshape(bf16[2,128,4,1536]{3,2,1,0:T(4,128)(2,1)} %copy.75) | data formatting | bytes 6291456 | tf_op jit(solution)/shard_map/all_to_all | solution.py:72
  269.4 41.7 %reduce-scatter.2.cloned.1.call-done = bf16[2,128,3072]{2,1,0:T(8,128)(2,1)} async-done(((bf16[2,128,6144]{2,1,0:T(8,128)(2,1)}), bf16[2,128,3072]{2,1,0:T(8,128)(2,1)}) %reduce-scatter.2.cloned.1.call-update) | async-done | bytes 1572880 | tf_op jit(solution)/shard_map/reduce_scatter | solution.py:75
  311.1 2.9 multiply_convert_fusion
  (28 shorter events, 5.9 us)
Async XLA Ops:
  6.5 262.4 %copy-start = (f32[64,3072]{1,0:T(8,128)S(1)}, f32[64,3072]{1,0:T(8,128)}, u32[]{:S(2)}) copy-start(f32[64,3072]{1,0:T(8,128)} %param.26) | copy-start | bytes 2359300
  6.5 37.2 %all-gather.4.cloned.1.call-start = ((), (), s32[]{:S(2)}) async-start(), calls=%async_computation.2 | async-start | bytes 1572864 | tf_op jit(solution)/shard_map/all_gather | solution.py:41
  25.6 27.7 %all-gather.6.cloned.1.call-start = ((), (), s32[]{:S(2)}) async-start(), calls=%async_computation.3 | async-start | bytes 1572864 | tf_op jit(solution)/shard_map/all_gather | solution.py:42
  43.6 129.0 %all-gather.8.cloned.1.call-start = ((), (), s32[]{:S(2)}) async-start(), calls=%async_computation.4 | async-start | bytes 3932160 | tf_op jit(solution)/shard_map/all_gather | solution.py:68
  79.6 231.5 %reduce-scatter.2.cloned.1.call-start = ((), (), s32[]{:S(2)}) async-start(), calls=%async_computation.5 | async-start | bytes 4718592 | tf_op jit(solution)/shard_map/reduce_scatter | solution.py:75
  268.3 0.7 copy-start.5
Sparse Core Ops, SparseCore 0:
  25.7 10.8 all-gather.3
  43.7 9.5 all-gather.5
  79.7 92.8 all-gather.7
  268.4 42.6 reduce-scatter.1
where the time goes:
time: 322 us; the launch traced here: 321 us
  waiting for transfers between devices  144 us (45%)
  blocking collectives  108 us (34%)
  local copies, waits for them, and re-layouts  22.1 us (7%)
  matrix products  19.2 us (6%)
  between operations  13.2 us (4%)
  other arithmetic  12.9 us (4%)
    all_gather x1, waiting for transfers between devices, per_device(): lax.all_gather(attn, 'seq', axis=1, tiled=True)  93 us
    all_to_all x1, blocking collectives, per_device(): lax.all_to_all(columns.astype(jnp.bfloat16), 'seq', split_axis=1, concat_...  73.3 us
    reduce_scatter x1, waiting for transfers between devices, per_device(): lax.psum_scatter(partial_out.astype(jnp.bfloat16), 'tp', scatter_dimensio...  41.7 us
    all_gather x1, blocking collectives, per_device(): lax.all_gather(key_states, 'seq', axis=1, tiled=True)  18 us
    all_gather x1, blocking collectives, per_device(): lax.all_gather(value_states, 'seq', axis=1, tiled=True)  17 us
    all_to_all x2, local copies, waits for them, and re-layouts, per_device(): lax.all_to_all(columns.astype(jnp.bfloat16), 'seq', split_axis=1, concat_...  11 us
    all_gather x1, waiting for transfers between devices, per_device(): value_piece = lax.all_gather(span_rows[1], 'span', axis=0, tiled=True)  9.6 us
    dot_general x1, matrix products, per_device(): jnp.einsum('ctf,fo->cto', lax.all_gather(attn, 'seq', axis=1, tiled=True)...  8.06 us
  transfers between devices with their start and end apart: 4, of which 3 were waited for; matrix products, arithmetic and copies ran while one was open for 0% of the time, Pallas kernels for 0%

commit v1 on v0

--- a/solution.py
+++ b/solution.py
@@ -63,11 +63,11 @@
         .reshape(ch_dev, tok_dev, heads_local * head_size)
         .astype(jnp.bfloat16)
     )
+    convert_sheets_now = lambda frame_in: jnp.concatenate(
+        lax.all_to_all(jnp.stack([frame_in] * lax.axis_size("seq")), "seq", 0, 0), axis=1
+    )
     columns = jnp.einsum(
-        "ctf,fo->cto",
-        lax.all_gather(attn, "seq", axis=1, tiled=True),
-        out_weight,
-        preferred_element_type=jnp.float32,
+        "ctf,fo->cto", convert_sheets_now(attn), out_weight, preferred_element_type=jnp.float32
     )
     partial_out = lax.all_to_all(
         columns.astype(jnp.bfloat16), "seq", split_axis=1, concat_axis=2, tiled=True

time: 322 us -> 291 us (0.904)
  waiting for transfers between devices: 144 us -> 54 us
  blocking collectives: 108 us -> 174 us
    all_gather x1 -> x0, waiting for transfers between devices: 93 us -> none  [per_device(): lax.all_gather(attn, 'seq', axis=1, tiled=True)]
    all_to_all x0 -> x1, blocking collectives: none -> 67.5 us  [per_device(): lax.all_to_all(jnp.stack([frame_in] * lax.axis_size('seq')), 'seq', 0, 0)]
  transfers between devices with their start and end apart: 4 -> 3, of which waited for: 3 -> 2; matrix products, arithmetic and copies ran while one was open for 0% -> 0% of each run, Pallas kernels for 0% -> 0%
where the time goes in v1:
time: 291 us; the launch traced here: 290 us
  blocking collectives  174 us (60%)
  waiting for transfers between devices  54 us (19%)
  local copies, waits for them, and re-layouts  20.6 us (7%)
  matrix products  16.4 us (6%)
  between operations  13.2 us (5%)
  other arithmetic  11.4 us (4%)
    all_to_all x1, blocking collectives, per_device(): lax.all_to_all(columns.astype(jnp.bfloat16), 'seq', split_axis=1, concat_...  71.2 us
    all_to_all x1, blocking collectives, per_device(): lax.all_to_all(jnp.stack([frame_in] * lax.axis_size('seq')), 'seq', 0, 0)  67.5 us
    reduce_scatter x1, waiting for transfers between devices, per_device(): lax.psum_scatter(partial_out.astype(jnp.bfloat16), 'tp', scatter_dimensio...  44.4 us
    all_gather x1, blocking collectives, per_device(): lax.all_gather(key_states, 'seq', axis=1, tiled=True)  18 us
    all_gather x1, blocking collectives, per_device(): lax.all_gather(value_states, 'seq', axis=1, tiled=True)  17 us
    all_to_all x2, local copies, waits for them, and re-layouts, per_device(): lax.all_to_all(columns.astype(jnp.bfloat16), 'seq', split_axis=1, concat_...  11 us
    all_gather x1, waiting for transfers between devices, per_device(): value_piece = lax.all_gather(span_rows[1], 'span', axis=0, tiled=True)  9.6 us
  transfers between devices with their start and end apart: 3, of which 2 were waited for; matrix products, arithmetic and copies ran while one was open for 0% of the time, Pallas kernels for 0%

profile of v1, /device:TPU:0, one launch (start us, length us, event | category | flops | bytes accessed | tf_op | source)
XLA Modules:
  0.0 289.6 jit_solution(5124503000283532018)
XLA Ops:
  6.5 1.0 copy.37
  7.5 18.0 %all_gather.12 = bf16[2,512,2,128]{3,1,2,0:T(8,128)(2,1)} all-gather(bf16[2,128,2,128]{3,1,2,0:T(8,128)(2,1)S(1)} %copy.37), channel_id=1, replica_groups=mesh['rep'=2,'span'=2,'seq'=4,'tp'=2] {'seq'}, dimensions={1}, use_global_device_ids=true | all-gather | bytes 655360 | tf_op jit(solution)/shard_map/all_gather | solution.py:38
  25.6 0.9 copy.38
  26.5 17.0 %all_gather.14 = bf16[2,512,2,128]{3,1,2,0:T(8,128)(2,1)} all-gather(bf16[2,128,2,128]{3,1,2,0:T(8,128)(2,1)S(1)} %copy.38), channel_id=1, replica_groups=mesh['rep'=2,'span'=2,'seq'=4,'tp'=2] {'seq'}, dimensions={1}, use_global_device_ids=true | all-gather | bytes 655360 | tf_op jit(solution)/shard_map/all_gather | solution.py:39
  43.7 9.6 %all-gather.5.cloned.1.call-done = bf16[4,512,2,128]{3,1,2,0:T(8,128)(2,1)} async-done(((bf16[2,512,2,128]{3,1,2,0:T(8,128)(2,1)}), bf16[4,512,2,128]{3,1,2,0:T(8,128)(2,1)}) %all-gather.5.cloned.1.call-update) | async-done | bytes 1048592 | tf_op jit(solution)/shard_map/all_gather | solution.py:42
  53.3 6.1 %conditional.8 = (f32[128,2,6]{0,2,1:T(8,128)}, f32[128,2,6]{0,2,1:T(8,128)S(1)}, f32[128,2,6,128]{3,0,2,1:T(8,128)S(1)}) conditional(s32[]{:T(128)} %convert_element_type.68, () %tuple.87, (bf16[4,512,2,128]{3,1,2,0:T(8,128)(2,1)}, bf16[2,128,2,6,128]{4,1,3,2,0:T(8,128)(2,1)}, bf16[4,512,2,128]{3,1,2,0:T(8,128)(2,1)}) %tuple.174), branch_computations={%region_0.0_spmd, %region_1.0_spmd} | conditional | flops 409147392 | bytes 11210776 | solution.py:55
  53.3 1.7 bitcast_reduce_fusion
  55.6 1.2 fusion.2
  56.8 0.7 fusion.21
  57.5 1.9 fusion.10
  59.4 6.1 %conditional.12 = (f32[128,2,6]{0,2,1:T(8,128)}, f32[128,2,6]{0,2,1:T(8,128)S(1)}, f32[128,2,6,128]{3,0,2,1:T(8,128)S(1)}) conditional(s32[]{:T(128)} %convert_element_type.72, () %tuple.93, (bf16[4,512,2,128]{3,1,2,0:T(8,128)(2,1)}, bf16[2,128,2,6,128]{4,1,3,2,0:T(8,128)(2,1)}, bf16[4,512,2,128]{3,1,2,0:T(8,128)(2,1)}) %tuple.177), branch_computations={%region_16.0_spmd, %region_17.0_spmd} | conditional | flops 409147392 | bytes 11210776 | solution.py:55
  59.4 1.7 bitcast_reduce_fusion.4
  61.7 1.2 fusion.85
  62.9 0.7 fusion.104
  63.6 1.9 fusion.93
  65.5 6.2 %conditional.13 = ((f32[128,2,6]{0,2,1:T(8,128)}, f32[128,2,6]{0,2,1:T(8,128)S(1)}, f32[128,2,6,128]{3,0,2,1:T(8,128)S(1)})) conditional(s32[]{:T(128)} %convert_element_type.71, (f32[128,2,6]{0,2,1:T(8,128)}, f32[128,2,6]{0,2,1:T(8,128)S(1)}, f32[128,2,6,128]{3,0,2,1:T(8,128)S(1)}) %conditional.12, (f32[128,2,6]{0,2,1:T(8,128)}, ...), branch_computations={%region_20.0_spmd, %region_21.0_spmd} | conditional | flops 409344000 | bytes 12032032 | solution.py:55
  65.5 1.7 bitcast_reduce_fusion.5
  68.4 0.7 multiply_add_fusion.4
  69.1 2.0 fusion.115
  71.8 1.2 conditional.11
  71.8 1.2 copy.39
  72.9 1.2 conditional.15
  72.9 1.2 copy.42
  74.1 1.5 fusion.171
  76.2 67.5 %all_to_all.23 = bf16[4,2,128,1536]{3,2,1,0:T(8,128)(2,1)S(1)} all-to-all(bf16[4,2,128,1536]{3,2,1,0:T(8,128)(2,1)S(1)} %stack.43), channel_id=1, replica_groups=mesh['rep'=2,'span'=2,'seq'=4,'tp'=2] {'seq'}, dimensions={0} | all-to-all | bytes 6291456 | tf_op jit(solution)/shard_map/all_to_all | solution.py:67
  144.0 5.3 %fusion.168 = bf16[2,512,1536]{2,1,0:T(8,128)(2,1)S(1)} fusion(bf16[2,512,1536]{2,1,0:T(8,128)(2,1)S(1)} %bitcast.331, bf16[1536,1536]{1,0:T(8,128)(2,1)S(1)} %bitcast.335), kind=kOutput, calls=%fused_computation.166 | convolution fusion | flops 4833411072 | bytes 11010048 | tf_op jit(solution)/shard_map/ctf,fo->cto/dot_general | solution.py:69
  149.2 3.2 %copy.47 = bf16[2,512,1536]{2,0,1:T(2,128)(2,1)S(1)} copy(bf16[2,512,1536]{2,1,0:T(8,128)(2,1)S(1)} %fusion.168) | data formatting | bytes 6291456 | tf_op jit(solution)/shard_map/convert_element_type | solution.py:73
  152.5 71.2 %all_to_all.24 = bf16[2,512,1536]{2,0,1:T(2,128)(2,1)S(1)} all-to-all(bf16[2,512,1536]{2,0,1:T(2,128)(2,1)S(1)} %copy.47), channel_id=1, replica_groups=mesh['rep'=2,'span'=2,'seq'=4,'tp'=2] {'seq'}, dimensions={1} | all-to-all | bytes 6291456 | tf_op jit(solution)/shard_map/all_to_all | solution.py:72
  223.7 4.1 %copy.48 = bf16[2,128,4,1536]{3,2,1,0:T(4,128)(2,1)} copy(bf16[2,128,4,1536]{3,0,1,2:T(2,128)(2,1)S(1)} %bitcast.330) | data formatting | bytes 6291456 | tf_op jit(solution)/shard_map/all_to_all | solution.py:72
  227.8 6.9 %all_to_all.20 = bf16[2,128,6144]{2,1,0:T(8,128)(2,1)} reshape(bf16[2,128,4,1536]{3,2,1,0:T(4,128)(2,1)} %copy.48) | data formatting | bytes 6291456 | tf_op jit(solution)/shard_map/all_to_all | solution.py:72
  235.8 44.4 %reduce-scatter.2.cloned.1.call-done = bf16[2,128,3072]{2,1,0:T(8,128)(2,1)} async-done(((bf16[2,128,6144]{2,1,0:T(8,128)(2,1)}), bf16[2,128,3072]{2,1,0:T(8,128)(2,1)}) %reduce-scatter.2.cloned.1.call-update) | async-done | bytes 1572880 | tf_op jit(solution)/shard_map/reduce_scatter | solution.py:75
  280.2 2.9 %multiply_convert_fusion = bf16[2,128,3072]{2,1,0:T(8,128)(2,1)} fusion(bf16[2,128,3072]{2,1,0:T(8,128)(2,1)} %reduce-scatter.2.cloned.1.call-done, f32[2,3072]{1,0:T(2,128)S(1)} %fusion.172), kind=kLoop, calls=%fused_computation.167 | loop fusion | flops 2359296 | bytes 3170304 | tf_op jit(solution)/shard_map/convert_element_type | solution.py:83
  (30 shorter events, 5.1 us)
Async XLA Ops:
  6.5 228.9 %copy-start = (f32[64,3072]{1,0:T(8,128)S(1)}, f32[64,3072]{1,0:T(8,128)}, u32[]{:S(2)}) copy-start(f32[64,3072]{1,0:T(8,128)} %param.26) | copy-start | bytes 2359300
  6.5 37.2 %all-gather.3.cloned.1.call-start = ((), (), s32[]{:S(2)}) async-start(), calls=%async_computation.3 | async-start | bytes 1572864 | tf_op jit(solution)/shard_map/all_gather | solution.py:41
  25.6 27.7 %all-gather.5.cloned.1.call-start = ((), (), s32[]{:S(2)}) async-start(), calls=%async_computation.4 | async-start | bytes 1572864 | tf_op jit(solution)/shard_map/all_gather | solution.py:42
  43.6 236.6 %reduce-scatter.2.cloned.1.call-start = ((), (), s32[]{:S(2)}) async-start(), calls=%async_computation.5 | async-start | bytes 4718592 | tf_op jit(solution)/shard_map/reduce_scatter | solution.py:75
  75.9 68.0 %slice-start = ((s8[4718592]{0:T(1024)(128)(4,1)}), s8[4194304]{0:T(1024)(128)(4,1)S(1)}, s32[]{:S(2)}) async-start(s8[4718592]{0:T(1024)(128)(4,1)} %bitcast.334), calls=%async_computation.6 | async-start | bytes 8388608
  76.2 67.8 %slice-start.1 = ((s8[4718592]{0:T(1024)(128)(4,1)}), s8[524288]{0:T(1024)(128)(4,1)S(1)}, s32[]{:S(2)}) async-start(s8[4718592]{0:T(1024)(128)(4,1)} %bitcast.334), calls=%async_computation.7 | async-start | bytes 1048576
  234.7 0.7 copy-start.5
Sparse Core Ops, SparseCore 0:
  25.7 10.8 all-gather.2
  43.7 9.5 all-gather.4
  234.9 45.2 reduce-scatter.1
